TPU v7x, 32 devices: a whole 2x2x4 slice. The times are simulated.
32 devices in a mesh: cells: 8 (over z, y), coef: 4 (over x, core).
Axes of the slice: x: 2, y: 2, z: 4, core: 2. Of those that a mesh axis runs over, the one named last changes fastest.
Arguments:
- multipole: bfloat16 [128, 1024], P('coef', 'cells'), may hold values from -6 to 6
- parent_local: bfloat16 [128, 128], P('coef', 'cells'), may hold values from -6 to 6
- m2l_ops: bfloat16 [189, 128, 128], P(None, 'coef'), may hold values from -0.0390625 to 0.0390625
- l2l_ops: bfloat16 [8, 128, 128], P(None, 'coef'), may hold values from -0.5 to 0.5
- target_cell: int32 [189, 1024], P(None, 'cells'), may hold values from -1 to 1023, as said below
- particle_leaf: int32 [16384], P('cells'), may hold values from 0 to 1023, as said below
- particle_basis: bfloat16 [128, 16384], P('coef', 'cells'), may hold values from -0.5 to 0.5
Outputs:
- leaf_local: float32 [128, 1024], P('coef', 'cells')
- potential: float32 [16384], P('cells')
Inputs may be any that keep to these rules, and one draw needn't show every extreme that they name: `target_cell`: -1 marks an empty slot. Otherwise the target of source cell c lies on the device of c (cells are owned in blocks of 128: device c // 128) or on a device at most 2 indices away; from one device's source cells at most 256 pairs target the cells of any one other device, and some pair of devices has exactly 256. `particle_leaf`: the particles at positions d * 2048 to (d + 1) * 2048 - 1 lie in cells d * 128 to (d + 1) * 128 - 1.
All inputs are finite; a program needn't handle non-finite values.
Results may differ from a plain program's by a relative error of at most 0.0003.
Values may be sent and summed in bfloat16 or wider, within the bound.
A program may use at most 64 MiB of HBM per device.

v0:
```python
import jax
import jax.numpy as jnp
from jax import lax
from jax.sharding import PartitionSpec as P

REACH = 2


def passed_along(value, axis, steps):
    count = lax.axis_size(axis)
    first, last = (max(0, -steps), min(count, count - steps))
    return lax.ppermute(value, axis, [(source, source + steps) for source in range(first, last)])


def on_device(
    multipole, parent_local, m2l_ops, l2l_ops, target_cell, particle_leaf, particle_basis
):
    my_index = lax.axis_index("cells")
    cells_dev = multipole.shape[1]
    full_poles, full_parents = (
        lax.all_gather(multipole, "coef", axis=0, tiled=True),
        lax.all_gather(parent_local, "coef", axis=0, tiled=True),
    )
    translated = jnp.einsum("oqk,kc->qoc", m2l_ops, full_poles, preferred_element_type=jnp.float32)
    coef_share = translated.shape[0]
    flat_terms = translated.reshape(coef_share, -1)
    targets = target_cell.reshape(-1)
    first_cell = my_index * cells_dev
    distances = []
    for length in range(1, REACH + 1):
        for direction in (1, -1):
            distances.append(length * direction)
    span = (2 * REACH + 1) * cells_dev
    lowest = (my_index - REACH) * cells_dev
    wide_index = jnp.where(targets >= 0, targets - lowest, span)
    wide_sums = (
        jnp.zeros((coef_share, span), jnp.float32).at[:, wide_index].add(flat_terms, mode="drop")
    )
    m2l_sum = wide_sums[:, REACH * cells_dev : (REACH + 1) * cells_dev]
    for distance in distances:
        offset = (REACH + distance) * cells_dev
        outgoing = wide_sums[:, offset : offset + cells_dev]
        m2l_sum = m2l_sum + passed_along(outgoing, "cells", distance)
    shifted = jnp.einsum("oqk,kp->qpo", l2l_ops, full_parents, preferred_element_type=jnp.float32)
    leaf_local = m2l_sum + shifted.reshape(coef_share, cells_dev)
    leaf_index = particle_leaf - first_cell
    columns = leaf_local[:, leaf_index]
    partial_sum = jnp.sum(columns * particle_basis.astype(jnp.float32), axis=0)
    potential = lax.psum(partial_sum, "coef")
    return (leaf_local, potential)


def solution(mesh):
    return jax.shard_map(
        on_device,
        mesh=mesh,
        in_specs=(
            P("coef", "cells"),
            P("coef", "cells"),
            P(None, "coef", None),
            P(None, "coef", None),
            P(None, "cells"),
            P("cells"),
            P("coef", "cells"),
        ),
        out_specs=(P("coef", "cells"), P("cells")),
        check_vma=False,
    )
```

profile of v0, /device:TPU:0, one launch (start us, length us, event | category | flops | bytes accessed | tf_op | source)
XLA Modules:
  0.0 183.9 jit_solution(15182055329372651720)
XLA Ops:
  0.6 0.0 copy-start
  0.7 1.0 select_bitcast_fusion
  1.7 0.3 fusion.5
  2.0 6.4 %all_gather.6 = bf16[128,128]{1,0:T(8,128)(2,1)S(1)} all-gather(bf16[32,128]{1,0:T(8,128)(2,1)} %param.7), channel_id=1, replica_groups=mesh['cells'=8,'coef'=4] {'coef'}, dimensions={0}, use_global_device_ids=true | all-gather | bytes 40960 | tf_op jit(solution)/shard_map/all_gather | solution.py:21
  8.4 0.0 copy-done
  8.4 0.7 fusion
  9.1 3.5 %copy.39 = f32[4,8,189,128]{3,1,2,0:T(8,128)} copy(f32[4,8,189,128]{3,2,1,0:T(8,128)S(1)} %bitcast.30) | data formatting | bytes 6193152
  12.6 0.0 copy-start.4
  12.6 0.0 copy-start.2
  12.6 0.0 copy-start.3
  12.6 7.7 %copy.27 = f32[24192,32]{1,0:T(8,128)} copy(f32[24192,32]{0,1:T(8,128)} %bitcast.31) | data formatting | bytes 6193152 | tf_op jit(solution)/shard_map/reshape | solution.py:26
  20.3 131.6 %scatter_custom_fusion = f32[32,640]{0,1:T(8,128)S(1)} fusion(s32[24192]{0:T(1024)S(1)} %fusion.5, f32[24192,32]{1,0:T(8,128)} %copy.27, f32[]{:T(128)} %constant.7.clone.1), kind=kCustom, calls=%fused_computation.9 | custom fusion | flops 774144 | bytes 82432 | tf_op jit(solution)/shard_map/scatter-add | solution.py:37
  151.9 3.9 %collective-permute-start = (f32[32,128]{0,1:T(8,128)S(1)}, f32[32,128]{0,1:T(8,128)S(1)}, u32[]{:S(2)}, u32[]{:S(2)}) collective-permute-start(f32[32,128]{0,1:T(8,128)S(1)} %get-tuple-element.10), channel_id=1, source_target_pairs={{0,4},{4,8},{8,12},{12,16},{16,20},{20,24},{24,28},{1,5},{5,9},{9,... | collective-permute-start | bytes 49160 | tf_op jit(solution)/shard_map/ppermute | solution.py:12
  155.8 1.3 collective-permute-start.1
  157.1 5.5 %collective-permute-start.2 = (f32[32,128]{0,1:T(8,128)S(1)}, f32[32,128]{0,1:T(8,128)S(1)}, u32[]{:S(2)}, u32[]{:S(2)}) collective-permute-start(f32[32,128]{0,1:T(8,128)S(1)} %get-tuple-element.12), channel_id=1, source_target_pairs={{0,8},{4,12},{8,16},{12,20},{16,24},{20,28},{1,9},{5,13},{9,17},{1... | collective-permute-start | bytes 49160 | tf_op jit(solution)/shard_map/ppermute | solution.py:12
  162.6 1.3 collective-permute-start.3
  163.9 0.0 copy-done.4
  164.0 5.2 %all-gather = bf16[4,32,16]{1,2,0:T(8,128)(2,1)S(1)} all-gather(bf16[1,32,16]{1,2,0:T(8,128)(2,1)S(1)} %bitcast.32), channel_id=1, replica_groups=mesh['cells'=8,'coef'=4] {'coef'}, dimensions={0}, use_global_device_ids=true | all-gather | bytes 5120 | tf_op jit(solution)/shard_map/all_gather | solution.py:22
  169.2 0.1 reshape.70
  169.3 0.0 copy-done.2
  169.3 0.2 convolution_bitcast_fusion
  169.4 0.0 copy-done.3
  169.5 0.0 collective-permute-done
  169.5 0.0 collective-permute-done.1
  169.5 0.0 collective-permute-done.2
  169.5 0.0 collective-permute-done.3
  169.6 0.7 copy.31
  170.2 5.5 %gather_fusion = f32[2048,32]{1,0:T(8,128)S(1)} fusion(f32[32,128]{0,1:T(8,128)S(1)} %fusion.9, s32[2048]{0:T(1024)S(1)} %fusion.11), kind=kCustom, calls=%fused_computation | custom fusion | bytes 532480 | tf_op jit(solution)/shard_map/gather | solution.py:47
  175.7 0.3 copy.30
  176.0 0.0 copy-done.1
  176.0 0.1 fusion.2
  176.1 7.8 %psum.7 = f32[2048]{0:T(1024)} all-reduce(f32[2048]{0:T(1024)S(1)} %fusion.2), channel_id=1, replica_groups=mesh['cells'=8,'coef'=4] {'coef'}, use_global_device_ids=true, to_apply=%region_2.3 | all-reduce | flops 2048 | bytes 16384 | tf_op jit(solution)/shard_map/psum | solution.py:49
  (5 shorter events, 0.1 us)
Async XLA Ops:
  0.6 7.8 %copy-start = (bf16[189,32,128]{2,1,0:T(8,128)(2,1)S(1)}, bf16[189,32,128]{2,1,0:T(8,128)(2,1)}, u32[]{:S(2)}) copy-start(bf16[189,32,128]{2,1,0:T(8,128)(2,1)} %param.9) | copy-start | bytes 4644868
  12.6 151.4 %copy-start.4 = (bf16[32,16]{0,1:T(8,128)(2,1)S(1)}, bf16[32,16]{0,1:T(8,128)(2,1)}, u32[]{:S(2)}) copy-start(bf16[32,16]{0,1:T(8,128)(2,1)} %param.8) | copy-start | bytes 3076
  12.6 156.7 %copy-start.2 = (bf16[8,32,128]{2,1,0:T(8,128)(2,1)S(1)}, bf16[8,32,128]{2,1,0:T(8,128)(2,1)}, u32[]{:S(2)}) copy-start(bf16[8,32,128]{2,1,0:T(8,128)(2,1)} %param.10) | copy-start | bytes 196612
  12.6 156.9 %copy-start.3 = (s32[2048]{0:T(1024)S(1)}, s32[2048]{0:T(1024)}, u32[]{:S(2)}) copy-start(s32[2048]{0:T(1024)} %param.12) | copy-start | bytes 24580
  20.3 155.7 %copy-start.1 = (bf16[32,2048]{1,0:T(8,128)(2,1)S(1)}, bf16[32,2048]{1,0:T(8,128)(2,1)}, u32[]{:S(2)}) copy-start(bf16[32,2048]{1,0:T(8,128)(2,1)} %param.13) | copy-start | bytes 393220
  151.9 17.5 %collective-permute-start = (f32[32,128]{0,1:T(8,128)S(1)}, f32[32,128]{0,1:T(8,128)S(1)}, u32[]{:S(2)}, u32[]{:S(2)}) collective-permute-start(f32[32,128]{0,1:T(8,128)S(1)} %get-tuple-element.10), channel_id=1, source_target_pairs={{0,4},{4,8},{8,12},{12,16},{16,20},{20,24},{24,28},{1,5},{5,9},{9,... | collective-permute-start | bytes 49160 | tf_op jit(solution)/shard_map/ppermute | solution.py:12
  155.8 13.7 %collective-permute-start.1 = (f32[32,128]{0,1:T(8,128)S(1)}, f32[32,128]{0,1:T(8,128)S(1)}, u32[]{:S(2)}, u32[]{:S(2)}) collective-permute-start(f32[32,128]{0,1:T(8,128)S(1)} %get-tuple-element.13), channel_id=1, source_target_pairs={{4,0},{8,4},{12,8},{16,12},{20,16},{24,20},{28,24},{5,1},{9,5},{13... | collective-permute-start | bytes 49160 | tf_op jit(solution)/shard_map/ppermute | solution.py:12
  157.1 12.4 %collective-permute-start.2 = (f32[32,128]{0,1:T(8,128)S(1)}, f32[32,128]{0,1:T(8,128)S(1)}, u32[]{:S(2)}, u32[]{:S(2)}) collective-permute-start(f32[32,128]{0,1:T(8,128)S(1)} %get-tuple-element.12), channel_id=1, source_target_pairs={{0,8},{4,12},{8,16},{12,20},{16,24},{20,28},{1,9},{5,13},{9,17},{1... | collective-permute-start | bytes 49160 | tf_op jit(solution)/shard_map/ppermute | solution.py:12
  162.6 6.9 %collective-permute-start.3 = (f32[32,128]{0,1:T(8,128)S(1)}, f32[32,128]{0,1:T(8,128)S(1)}, u32[]{:S(2)}, u32[]{:S(2)}) collective-permute-start(f32[32,128]{0,1:T(8,128)S(1)} %get-tuple-element.11), channel_id=1, source_target_pairs={{8,0},{12,4},{16,8},{20,12},{24,16},{28,20},{9,1},{13,5},{17,9},{2... | collective-permute-start | bytes 49160 | tf_op jit(solution)/shard_map/ppermute | solution.py:12
where the time goes:
time: 184 us
  other arithmetic  133 us (72%)
  blocking collectives  19.4 us (11%)
  local copies, waits for them, and re-layouts  17.8 us (10%)
  starting transfers between devices  12 us (7%)
    scatter-add x1, other arithmetic, on_device(): jnp.zeros((coef_share, span), jnp.float32).at[:, wide_index]  132 us
    ppermute x4, starting transfers between devices, passed_along(): lax.ppermute(value, axis, [(source, source + steps) for source in range(f...  12 us
    psum x1, blocking collectives, on_device(): potential = lax.psum(partial_sum, 'coef')  7.78 us
    reshape x1, local copies, waits for them, and re-layouts, on_device(): flat_terms = translated.reshape(coef_share, -1)  7.75 us
    all_gather x1, blocking collectives, on_device(): lax.all_gather(multipole, 'coef', axis=0, tiled=True)  6.42 us
    gather x2, local copies, waits for them, and re-layouts, on_device(): columns = leaf_local[:, leaf_index]  5.77 us
    all_gather x1, blocking collectives, on_device(): lax.all_gather(parent_local, 'coef', axis=0, tiled=True)  5.21 us
    unnamed x13, local copies, waits for them, and re-layouts  4.27 us
  transfers between devices with their start and end apart: 4, of which 0 were waited for; matrix products, arithmetic and copies ran while one was open for 0% of the time, Pallas kernels for 0%

commit v1 on v0

v1 whole, which is shorter than its diff:
```python
import functools

import jax
import jax.numpy as jnp
from jax import lax
from jax.experimental import pallas as pl
from jax.experimental.pallas import tpu as pltpu
from jax.sharding import PartitionSpec as P

REACH = 2
WINDOWS = tuple(w for r in range(REACH, 0, -1) for w in (-r, r))
GROUP = 16
NT = (((1,), (1,)), ((), ()))


def halves(value):
    high = value.astype(jnp.bfloat16)
    low = (value - high.astype(jnp.float32)).astype(jnp.bfloat16)
    return high, low


def kernel(
    n_cells, n_coef,
    mine_ref, ops_hbm, l2l_hbm, target_hbm, leaf_hbm, basis_hbm,
    local_ref, pot_ref,
    ops_ref, l2l_ref, target_ref, leaf_ref, basis_ref,
    gathered, pieces, out_buf, in_buf, total, partials,
    load_sem, g_send, g_recv, w_send, w_recv, p_send, p_recv,
):
    row = lax.axis_index("cells")
    col = lax.axis_index("coef")
    noff, share, width = ops_ref.shape
    cd = target_ref.shape[1]
    tiles = leaf_ref.shape[0]
    lanes = leaf_ref.shape[1]

    loads = [
        pltpu.make_async_copy(src, dst, load_sem.at[i])
        for i, (src, dst) in enumerate(
            ((target_hbm, target_ref), (ops_hbm, ops_ref), (l2l_hbm, l2l_ref),
             (leaf_hbm, leaf_ref), (basis_hbm, basis_ref))
        )
    ]
    for load in loads:
        load.start()

    barrier = pltpu.get_barrier_semaphore()
    for d in range(1, n_coef):
        pl.semaphore_signal(
            barrier, inc=1, device_id=(row, lax.rem(col + d, n_coef)),
            device_id_type=pl.DeviceIdType.MESH,
        )
    for w in WINDOWS:
        @pl.when((row + w >= 0) & (row + w < n_cells))
        def _():
            pl.semaphore_signal(
                barrier, inc=1, device_id=(row + w, col), device_id_type=pl.DeviceIdType.MESH
            )
    peers = n_coef - 1
    for w in WINDOWS:
        peers = peers + ((row + w >= 0) & (row + w < n_cells)).astype(jnp.int32)
    pl.semaphore_wait(barrier, peers)

    def gather_copy(d):
        return pltpu.make_async_remote_copy(
            src_ref=mine_ref, dst_ref=gathered.at[col],
            send_sem=g_send.at[d - 1], recv_sem=g_recv.at[col],
            device_id=(row, lax.rem(col + d, n_coef)), device_id_type=pl.DeviceIdType.MESH,
        )

    def gather_arrival(d):
        source = lax.rem(col + d, n_coef)
        return pltpu.make_async_remote_copy(
            src_ref=mine_ref, dst_ref=gathered.at[source],
            send_sem=g_send.at[d - 1], recv_sem=g_recv.at[source],
            device_id=(row, source), device_id_type=pl.DeviceIdType.MESH,
        )

    for d in range(1, n_coef):
        gather_copy(d).start()
    gathered[col] = mine_ref[...]
    loads[0].wait()
    loads[1].wait()
    for d in range(1, n_coef):
        gather_arrival(d).wait_recv()

    poles = jnp.concatenate([gathered[j, :, :cd] for j in range(n_coef)], axis=0)
    iota = lax.broadcasted_iota(jnp.int32, (cd, cd), 0).astype(jnp.float32).astype(jnp.bfloat16)
    one = jnp.ones((cd, cd), jnp.bfloat16)
    zero = jnp.zeros((cd, cd), jnp.bfloat16)

    def one_hot(line):
        wide = jnp.broadcast_to(line.astype(jnp.float32), (16, line.shape[1])).astype(jnp.bfloat16)
        tall = jnp.concatenate([wide] * (cd // 16), axis=0)
        return jnp.where(tall == iota, one, zero)

    def lines(first, count):
        result = []
        for j in range(count):
            line = target_ref[pl.ds(first + j, 1), :]
            result.append(jnp.where(line >= 0, line - row * cd, -8 * REACH * cd))
        return result

    def span(first, count):
        return pl.ds(pl.multiple_of(first * cd, cd), count * cd)

    def far(first, count):
        block = ops_ref[pl.ds(first, count)].reshape(count * share, width)
        terms = jnp.dot(block, poles, preferred_element_type=jnp.float32)
        high, low = halves(terms)
        both = jnp.concatenate(
            [
                jnp.concatenate([part[j * share : (j + 1) * share] for j in range(count)], axis=1)
                for part in (high, low)
            ],
            axis=0,
        )
        pieces[:, span(first, count)] = both
        rows = lines(first, count)
        hot = jnp.concatenate(
            [
                jnp.concatenate([one_hot(line - w * cd) for line in rows], axis=1)
                for w in WINDOWS
            ],
            axis=0,
        )
        return lax.dot_general(both, hot, NT, preferred_element_type=jnp.float32)

    def near(first, count):
        hot = jnp.concatenate([one_hot(line) for line in lines(first, count)], axis=1)
        return lax.dot_general(
            pieces[:, span(first, count)], hot, NT, preferred_element_type=jnp.float32
        )

    def over_offsets(step, columns):
        full = noff // GROUP
        acc = jnp.zeros((2 * share, columns), jnp.float32)
        acc = lax.fori_loop(0, full, lambda i, a: a + step(i * GROUP, GROUP), acc)
        if noff % GROUP:
            acc = acc + step(full * GROUP, noff % GROUP)
        return acc[:share] + acc[share:]

    def window_copy(i, w):
        return pltpu.make_async_remote_copy(
            src_ref=out_buf.at[i], dst_ref=in_buf.at[i],
            send_sem=w_send.at[i], recv_sem=w_recv.at[i],
            device_id=(row + w, col), device_id_type=pl.DeviceIdType.MESH,
        )

    sums = over_offsets(far, len(WINDOWS) * cd)
    for i, w in enumerate(WINDOWS):
        out_buf[i] = sums[:, i * cd : (i + 1) * cd]
    for i, w in enumerate(WINDOWS):
        @pl.when((row + w >= 0) & (row + w < n_cells))
        def _():
            window_copy(i, w).start()

    total[...] = over_offsets(near, cd)

    loads[2].wait()
    parents = jnp.concatenate([gathered[j, :, cd:] for j in range(n_coef)], axis=0)
    octant = lax.broadcasted_iota(jnp.int32, parents.shape, 1) % 8
    wide_parents = parents.astype(jnp.float32)
    spread = jnp.concatenate(
        [jnp.where(octant == j, wide_parents, 0.0).astype(jnp.bfloat16) for j in range(8)], axis=0
    )
    shifts = jnp.concatenate([l2l_ref[j] for j in range(8)], axis=1)
    total[...] += jnp.dot(shifts, spread, preferred_element_type=jnp.float32)

    loads[3].wait()
    leaf_hot = jnp.concatenate(
        [one_hot(leaf_ref[t : t + 1, :] - row * cd) for t in range(tiles)], axis=1
    )
    loads[4].wait()

    for i, w in enumerate(WINDOWS):
        @pl.when((row - w >= 0) & (row - w < n_cells))
        def _():
            window_copy(i, w).wait_recv()
            total[...] += in_buf[i]

    local = total[...]
    local_ref[...] = local
    columns = jnp.dot(
        jnp.concatenate(halves(local), axis=0), leaf_hot, preferred_element_type=jnp.float32
    )
    columns = columns[:share] + columns[share:]
    partial = jnp.sum(columns * basis_ref[...].astype(jnp.float32), axis=0, keepdims=True)
    partials[col] = jnp.concatenate(
        [partial[:, t * lanes : (t + 1) * lanes] for t in range(tiles)], axis=0
    )

    def partial_copy(d, slot):
        return pltpu.make_async_remote_copy(
            src_ref=partials.at[slot], dst_ref=partials.at[slot],
            send_sem=p_send.at[d - 1], recv_sem=p_recv.at[slot],
            device_id=(row, lax.rem(col + d, n_coef)), device_id_type=pl.DeviceIdType.MESH,
        )

    for d in range(1, n_coef):
        partial_copy(d, col).start()
    for d in range(1, n_coef):
        partial_copy(d, lax.rem(col + d, n_coef)).wait_recv()
    potential = partials[0]
    for j in range(1, n_coef):
        potential = potential + partials[j]
    pot_ref[...] = potential

    for d in range(1, n_coef):
        gather_copy(d).wait_send()
        partial_copy(d, col).wait_send()
    for i, w in enumerate(WINDOWS):
        @pl.when((row + w >= 0) & (row + w < n_cells))
        def _():
            window_copy(i, w).wait_send()


def on_device(
    n_cells, n_coef,
    multipole, parent_local, m2l_ops, l2l_ops, target_cell, particle_leaf, particle_basis,
):
    share, cd = multipole.shape
    noff = m2l_ops.shape[0]
    width = m2l_ops.shape[2]
    particles = particle_leaf.shape[0]
    lanes = 128
    tiles = particles // lanes
    mine = jnp.concatenate([multipole, jnp.repeat(parent_local, 8, axis=1)], axis=1)
    leaf = particle_leaf.reshape(tiles, lanes)
    nwin = len(WINDOWS)
    dma = pltpu.SemaphoreType.DMA
    vmem = pl.BlockSpec(memory_space=pltpu.VMEM)
    anywhere = pl.BlockSpec(memory_space=pl.ANY)
    local, potential = pl.pallas_call(
        functools.partial(kernel, n_cells, n_coef),
        out_shape=(
            jax.ShapeDtypeStruct((share, cd), jnp.float32),
            jax.ShapeDtypeStruct((tiles, lanes), jnp.float32),
        ),
        in_specs=[vmem] + [anywhere] * 5,
        out_specs=(vmem, vmem),
        scratch_shapes=[
            pltpu.VMEM(m2l_ops.shape, m2l_ops.dtype),
            pltpu.VMEM(l2l_ops.shape, l2l_ops.dtype),
            pltpu.VMEM(target_cell.shape, target_cell.dtype),
            pltpu.VMEM(leaf.shape, leaf.dtype),
            pltpu.VMEM(particle_basis.shape, particle_basis.dtype),
            pltpu.VMEM((n_coef, share, 2 * cd), jnp.bfloat16),
            pltpu.VMEM((2 * share, noff * cd), jnp.bfloat16),
            pltpu.VMEM((nwin, share, cd), jnp.float32),
            pltpu.VMEM((nwin, share, cd), jnp.float32),
            pltpu.VMEM((share, cd), jnp.float32),
            pltpu.VMEM((n_coef, tiles, lanes), jnp.float32),
            dma((5,)),
            dma((n_coef - 1,)),
            dma((n_coef,)),
            dma((nwin,)),
            dma((nwin,)),
            dma((n_coef - 1,)),
            dma((n_coef,)),
        ],
        compiler_params=pltpu.CompilerParams(
            collective_id=0, has_side_effects=True, vmem_limit_bytes=48 * 1024 * 1024
        ),
    )(mine, m2l_ops, l2l_ops, target_cell, leaf, particle_basis)
    return local, potential.reshape(particles)


def solution(mesh):
    return jax.shard_map(
        functools.partial(on_device, mesh.shape["cells"], mesh.shape["coef"]),
        mesh=mesh,
        in_specs=(
            P("coef", "cells"),
            P("coef", "cells"),
            P(None, "coef", None),
            P(None, "coef", None),
            P(None, "cells"),
            P("cells"),
            P("coef", "cells"),
        ),
        out_specs=(P("coef", "cells"), P("cells")),
        check_vma=False,
    )
```

time: 184 us -> 32 us (0.17)
  other arithmetic: 133 us -> 0.73 us
  Pallas kernels: 0 us -> 23.6 us
  blocking collectives: 19.4 us -> 0 us
  starting transfers between devices: 12 us -> 0 us
  local copies, waits for them, and re-layouts: 17.8 us -> 6.7 us
    scatter-add x1 -> x0, other arithmetic: 132 us -> none  [on_device(): jnp.zeros((coef_share, span), jnp.float32).at[:, wide_index]]
    pallas_call x0 -> x1, Pallas kernels: none -> 23.6 us  [on_device(): pl.pallas_call(functools.partial(kernel, n_cells, n_coef), out_shape=(jax...]
    ppermute x4 -> x0, starting transfers between devices: 12 us -> none  [passed_along(): lax.ppermute(value, axis, [(source, source + steps) for source in range(f...]
    all_gather x2 -> x0, blocking collectives: 11.6 us -> none  [the longest x1 6.42 us: on_device(): lax.all_gather(multipole, 'coef', axis=0, tiled=True)]
    psum x1 -> x0, blocking collectives: 7.78 us -> none  [on_device(): potential = lax.psum(partial_sum, 'coef')]
    reshape x1 -> x2, local copies, waits for them, and re-layouts: 7.75 us -> 0.07 us  [on_device(): jnp.repeat(parent_local, 8, axis=1)]
    gather x2 -> x0, local copies, waits for them, and re-layouts: 5.77 us -> none  [on_device(): columns = leaf_local[:, leaf_index]]
    unnamed x13 -> x14, local copies, waits for them, and re-layouts: 4.27 us -> 6.62 us
  transfers between devices with their start and end apart: 4 -> 0, of which waited for: 0 -> 0; matrix products, arithmetic and copies ran while one was open for 0% -> 0% of each run, Pallas kernels for 0% -> 0%
where the time goes in v1:
time: 32 us; the launch traced here: 31.7 us
  Pallas kernels  23.6 us (74%)
  local copies, waits for them, and re-layouts  6.7 us (21%)
  other arithmetic  0.73 us (2%)
  between operations  0.65 us (2%)
    pallas_call x1, Pallas kernels, on_device(): pl.pallas_call(functools.partial(kernel, n_cells, n_coef), out_shape=(jax...  23.6 us
    unnamed x14, local copies, waits for them, and re-layouts  6.62 us
    concatenate x1, other arithmetic, on_device(): jnp.concatenate([multipole, jnp.repeat(parent_local, 8, axis=1)], axis=1)  0.73 us

profile of v1, /device:TPU:0, one launch (start us, length us, event | category | flops | bytes accessed | tf_op | source)
XLA Modules:
  0.0 31.7 jit_solution(66352613581281428)
XLA Ops:
  0.6 0.0 copy-start
  0.6 0.7 %copy-done = bf16[32,16]{0,1:T(8,128)(2,1)S(1)} copy-done((bf16[32,16]{0,1:T(8,128)(2,1)S(1)}, bf16[32,16]{0,1:T(8,128)(2,1)}, u32[]{:S(2)}) %copy-start) | copy-done | bytes 1048
  1.3 0.1 copy.10
  1.4 0.7 %pad_maximum_fusion.mine_ref = bf16[32,256]{1,0:T(8,128)(2,1)S(1)} fusion(bf16[32,128]{1,0:T(8,128)(2,1)S(1)} %copy.10, bf16[32,128]{1,0:T(8,128)(2,1)} %param.7), kind=kLoop, calls=%fused_computation | loop fusion | flops 32768 | bytes 32768 | tf_op jit(solution)/shard_map/concatenate | solution.py:228
  2.1 0.0 copy-start.1
  2.1 1.4 %copy-done.1 = bf16[189,32,128]{2,1,0:T(8,128)(2,1)S(1)} copy-done((bf16[189,32,128]{2,1,0:T(8,128)(2,1)S(1)}, bf16[189,32,128]{2,1,0:T(8,128)(2,1)}, u32[]{:S(2)}) %copy-start.1) | copy-done | bytes 1548312
  3.5 0.0 copy-start.2
  3.5 0.9 %copy-done.2 = bf16[32,2048]{1,0:T(8,128)(2,1)S(1)} copy-done((bf16[32,2048]{1,0:T(8,128)(2,1)S(1)}, bf16[32,2048]{1,0:T(8,128)(2,1)}, u32[]{:S(2)}) %copy-start.2) | copy-done | bytes 131096
  4.4 0.0 copy-start.3
  4.4 0.9 %copy-done.3 = s32[189,128]{1,0:T(8,128)S(1)} copy-done((s32[189,128]{1,0:T(8,128)S(1)}, s32[189,128]{1,0:T(8,128)}, u32[]{:S(2)}) %copy-start.3) | copy-done | bytes 96792
  5.3 0.0 copy-start.4
  5.3 0.8 %copy-done.4 = bf16[8,32,128]{2,1,0:T(8,128)(2,1)S(1)} copy-done((bf16[8,32,128]{2,1,0:T(8,128)(2,1)S(1)}, bf16[8,32,128]{2,1,0:T(8,128)(2,1)}, u32[]{:S(2)}) %copy-start.4) | copy-done | bytes 65560
  6.2 0.0 copy-start.5
  6.2 0.7 %copy-done.5 = s32[2048]{0:T(1024)S(1)} copy-done((s32[2048]{0:T(1024)S(1)}, s32[2048]{0:T(1024)}, u32[]{:S(2)}) %copy-start.5) | copy-done | bytes 8216
  6.9 23.6 %shard_map.86 = (f32[32,128]{1,0:T(8,128)S(1)}, f32[16,128]{1,0:T(8,128)S(1)}) custom-call(bf16[32,256]{1,0:T(8,128)(2,1)S(1)} %pad_maximum_fusion.mine_ref, bf16[189,32,128]{2,1,0:T(8,128)(2,1)S(1)} %copy-done.1, bf16[8,32,128]{2,1,0:T(8,128)(2,1)S(1)} %copy-done.4, s32[189,128]{1,0:T(8,128)S(1)} %copy-done.3, s32[16,128]{1,0:T(8,128)S(1)} %bitcast.4, ...), custom_call_target="tpu_custom_call" | custom-call | tf_op jit(solution)/shard_map/pallas_call | solution.py:234
  30.5 0.6 %copy.13 = f32[32,128]{1,0:T(8,128)} copy(f32[32,128]{1,0:T(8,128)S(1)} %get-tuple-element.8) | data formatting | bytes 32768
  31.1 0.6 %copy.14 = f32[2048]{0:T(1024)} copy(f32[2048]{0:T(1024)S(1)} %bitcast.5) | data formatting | bytes 16384
  (1 shorter events, 0.0 us)
Async XLA Ops:
  0.6 0.7 %copy-start = (bf16[32,16]{0,1:T(8,128)(2,1)S(1)}, bf16[32,16]{0,1:T(8,128)(2,1)}, u32[]{:S(2)}) copy-start(bf16[32,16]{0,1:T(8,128)(2,1)} %param.8) | copy-start | bytes 3076
  2.1 1.4 %copy-start.1 = (bf16[189,32,128]{2,1,0:T(8,128)(2,1)S(1)}, bf16[189,32,128]{2,1,0:T(8,128)(2,1)}, u32[]{:S(2)}) copy-start(bf16[189,32,128]{2,1,0:T(8,128)(2,1)} %ops_hbm.1) | copy-start | bytes 4644868
  3.5 0.9 %copy-start.2 = (bf16[32,2048]{1,0:T(8,128)(2,1)S(1)}, bf16[32,2048]{1,0:T(8,128)(2,1)}, u32[]{:S(2)}) copy-start(bf16[32,2048]{1,0:T(8,128)(2,1)} %basis_hbm.1) | copy-start | bytes 393220
  4.4 0.9 %copy-start.3 = (s32[189,128]{1,0:T(8,128)S(1)}, s32[189,128]{1,0:T(8,128)}, u32[]{:S(2)}) copy-start(s32[189,128]{1,0:T(8,128)} %target_hbm.1) | copy-start | bytes 290308
  5.3 0.8 %copy-start.4 = (bf16[8,32,128]{2,1,0:T(8,128)(2,1)S(1)}, bf16[8,32,128]{2,1,0:T(8,128)(2,1)}, u32[]{:S(2)}) copy-start(bf16[8,32,128]{2,1,0:T(8,128)(2,1)} %l2l_hbm.1) | copy-start | bytes 196612
  6.2 0.7 %copy-start.5 = (s32[2048]{0:T(1024)S(1)}, s32[2048]{0:T(1024)}, u32[]{:S(2)}) copy-start(s32[2048]{0:T(1024)} %param.12) | copy-start | bytes 24580

commit v2 on v1

--- a/solution.py
+++ b/solution.py
@@ -21,11 +21,11 @@
 
 def kernel(
     n_cells, n_coef,
-    mine_ref, ops_hbm, l2l_hbm, target_hbm, leaf_hbm, basis_hbm,
+    poles_hbm, parents_hbm, ops_hbm, l2l_hbm, target_hbm, leaf_hbm, basis_hbm,
     local_ref, pot_ref,
     ops_ref, l2l_ref, target_ref, leaf_ref, basis_ref,
-    gathered, pieces, out_buf, in_buf, total, partials,
-    load_sem, g_send, g_recv, w_send, w_recv, p_send, p_recv,
+    gathered, elders, pieces, out_buf, in_buf, total, partials,
+    load_sem, g_send, g_recv, e_send, e_recv, w_send, w_recv, p_send, p_recv,
 ):
     row = lax.axis_index("cells")
     col = lax.axis_index("coef")
@@ -38,7 +38,8 @@
         pltpu.make_async_copy(src, dst, load_sem.at[i])
         for i, (src, dst) in enumerate(
             ((target_hbm, target_ref), (ops_hbm, ops_ref), (l2l_hbm, l2l_ref),
-             (leaf_hbm, leaf_ref), (basis_hbm, basis_ref))
+             (leaf_hbm, leaf_ref), (basis_hbm, basis_ref),
+             (poles_hbm, gathered.at[col]), (parents_hbm, elders.at[col]))
         )
     ]
     for load in loads:
@@ -61,30 +62,26 @@
         peers = peers + ((row + w >= 0) & (row + w < n_cells)).astype(jnp.int32)
     pl.semaphore_wait(barrier, peers)
 
-    def gather_copy(d):
+    def gather_copy(k, d, slot):
+        src, dst, send, recv = (
+            (poles_hbm, gathered, g_send, g_recv), (parents_hbm, elders, e_send, e_recv)
+        )[k]
         return pltpu.make_async_remote_copy(
-            src_ref=mine_ref, dst_ref=gathered.at[col],
-            send_sem=g_send.at[d - 1], recv_sem=g_recv.at[col],
+            src_ref=src, dst_ref=dst.at[slot],
+            send_sem=send.at[d - 1], recv_sem=recv.at[slot],
             device_id=(row, lax.rem(col + d, n_coef)), device_id_type=pl.DeviceIdType.MESH,
         )
 
-    def gather_arrival(d):
-        source = lax.rem(col + d, n_coef)
-        return pltpu.make_async_remote_copy(
-            src_ref=mine_ref, dst_ref=gathered.at[source],
-            send_sem=g_send.at[d - 1], recv_sem=g_recv.at[source],
-            device_id=(row, source), device_id_type=pl.DeviceIdType.MESH,
-        )
-
-    for d in range(1, n_coef):
-        gather_copy(d).start()
-    gathered[col] = mine_ref[...]
+    for k in range(2):
+        for d in range(1, n_coef):
+            gather_copy(k, d, col).start()
+    loads[5].wait()
     loads[0].wait()
+    for d in range(1, n_coef):
+        gather_copy(0, d, lax.rem(col + d, n_coef)).wait_recv()
     loads[1].wait()
-    for d in range(1, n_coef):
-        gather_arrival(d).wait_recv()
-
-    poles = jnp.concatenate([gathered[j, :, :cd] for j in range(n_coef)], axis=0)
+
+    poles = jnp.concatenate([gathered[j] for j in range(n_coef)], axis=0)
     iota = lax.broadcasted_iota(jnp.int32, (cd, cd), 0).astype(jnp.float32).astype(jnp.bfloat16)
     one = jnp.ones((cd, cd), jnp.bfloat16)
     zero = jnp.zeros((cd, cd), jnp.bfloat16)
@@ -158,9 +155,23 @@
     total[...] = over_offsets(near, cd)
 
     loads[2].wait()
-    parents = jnp.concatenate([gathered[j, :, cd:] for j in range(n_coef)], axis=0)
-    octant = lax.broadcasted_iota(jnp.int32, parents.shape, 1) % 8
-    wide_parents = parents.astype(jnp.float32)
+    loads[6].wait()
+    for d in range(1, n_coef):
+        gather_copy(1, d, lax.rem(col + d, n_coef)).wait_recv()
+    held = (elders.shape[1], cd)
+    child = lax.broadcasted_iota(jnp.int32, held, 1)
+    family = child // 8 == lax.broadcasted_iota(jnp.int32, held, 0)
+    family = family.astype(jnp.float32).astype(jnp.bfloat16)
+    wide_parents = jnp.concatenate(
+        [
+            lax.dot_general(
+                elders[j], family, (((0,), (0,)), ((), ())), preferred_element_type=jnp.float32
+            )
+            for j in range(n_coef)
+        ],
+        axis=0,
+    )
+    octant = lax.broadcasted_iota(jnp.int32, wide_parents.shape, 1) % 8
     spread = jnp.concatenate(
         [jnp.where(octant == j, wide_parents, 0.0).astype(jnp.bfloat16) for j in range(8)], axis=0
     )
@@ -207,7 +218,8 @@
     pot_ref[...] = potential
 
     for d in range(1, n_coef):
-        gather_copy(d).wait_send()
+        gather_copy(0, d, col).wait_send()
+        gather_copy(1, d, col).wait_send()
         partial_copy(d, col).wait_send()
     for i, w in enumerate(WINDOWS):
         @pl.when((row + w >= 0) & (row + w < n_cells))
@@ -225,19 +237,18 @@
     particles = particle_leaf.shape[0]
     lanes = 128
     tiles = particles // lanes
-    mine = jnp.concatenate([multipole, jnp.repeat(parent_local, 8, axis=1)], axis=1)
     leaf = particle_leaf.reshape(tiles, lanes)
     nwin = len(WINDOWS)
     dma = pltpu.SemaphoreType.DMA
     vmem = pl.BlockSpec(memory_space=pltpu.VMEM)
-    anywhere = pl.BlockSpec(memory_space=pl.ANY)
+    hbm = pl.BlockSpec(memory_space=pltpu.HBM)
     local, potential = pl.pallas_call(
         functools.partial(kernel, n_cells, n_coef),
         out_shape=(
             jax.ShapeDtypeStruct((share, cd), jnp.float32),
             jax.ShapeDtypeStruct((tiles, lanes), jnp.float32),
         ),
-        in_specs=[vmem] + [anywhere] * 5,
+        in_specs=[hbm] * 7,
         out_specs=(vmem, vmem),
         scratch_shapes=[
             pltpu.VMEM(m2l_ops.shape, m2l_ops.dtype),
@@ -245,13 +256,16 @@
             pltpu.VMEM(target_cell.shape, target_cell.dtype),
             pltpu.VMEM(leaf.shape, leaf.dtype),
             pltpu.VMEM(particle_basis.shape, particle_basis.dtype),
-            pltpu.VMEM((n_coef, share, 2 * cd), jnp.bfloat16),
+            pltpu.VMEM((n_coef, share, cd), jnp.bfloat16),
+            pltpu.VMEM((n_coef,) + parent_local.shape[::-1], jnp.bfloat16),
             pltpu.VMEM((2 * share, noff * cd), jnp.bfloat16),
             pltpu.VMEM((nwin, share, cd), jnp.float32),
             pltpu.VMEM((nwin, share, cd), jnp.float32),
             pltpu.VMEM((share, cd), jnp.float32),
             pltpu.VMEM((n_coef, tiles, lanes), jnp.float32),
-            dma((5,)),
+            dma((7,)),
+            dma((n_coef - 1,)),
+            dma((n_coef,)),
             dma((n_coef - 1,)),
             dma((n_coef,)),
             dma((nwin,)),
@@ -260,9 +274,9 @@
             dma((n_coef,)),
         ],
         compiler_params=pltpu.CompilerParams(
-            collective_id=0, has_side_effects=True, vmem_limit_bytes=48 * 1024 * 1024
+            collective_id=0, has_side_effects=True, vmem_limit_bytes=67043328
         ),
-    )(mine, m2l_ops, l2l_ops, target_cell, leaf, particle_basis)
+    )(multipole, parent_local.T, m2l_ops, l2l_ops, target_cell, leaf, particle_basis)
     return local, potential.reshape(particles)
 
 

time: 32 us -> 27.4 us (0.86)
  local copies, waits for them, and re-layouts: 6.7 us -> 2.62 us
  other arithmetic: 0.73 us -> 0 us
    unnamed x14 -> x2, local copies, waits for them, and re-layouts: 6.62 us -> 2.62 us
    concatenate x1 -> x0, other arithmetic: 0.73 us -> none  [on_device(): jnp.concatenate([multipole, jnp.repeat(parent_local, 8, axis=1)], axis=1)]
where the time goes in v2:
time: 27.4 us; the launch traced here: 27.1 us
  Pallas kernels  23.9 us (87%)
  local copies, waits for them, and re-layouts  2.62 us (10%)
  between operations  0.64 us (2%)
    pallas_call x1, Pallas kernels, on_device(): pl.pallas_call(functools.partial(kernel, n_cells, n_coef), out_shape=(jax...  23.9 us
    unnamed x2, local copies, waits for them, and re-layouts  2.62 us

profile of v2, /device:TPU:0, one launch (start us, length us, event | category | flops | bytes accessed | tf_op | source)
XLA Modules:
  0.0 27.1 jit_solution(7928806003683887727)
XLA Ops:
  0.6 23.9 %shard_map.86 = (f32[32,128]{1,0:T(8,128)}, f32[16,128]{1,0:T(8,128)}) custom-call(bf16[32,128]{1,0:T(8,128)(2,1)} %poles_hbm.1, bf16[16,32]{1,0:T(8,128)(2,1)} %bitcast.5, bf16[189,32,128]{2,1,0:T(8,128)(2,1)} %ops_hbm.1, bf16[8,32,128]{2,1,0:T(8,128)(2,1)} %l2l_hbm.1, s32[189,128]{1,0:T(8,128)} %target_hbm.1, s32[16,128]{1,0:T(8,128)} %bitcast.3, ...), custom_call_target="tpu_custom_call" | custom-call | tf_op jit(solution)/shard_map/pallas_call | solution.py:245
  24.5 1.3 %copy.11 = f32[32,128]{1,0:T(8,128)} copy(f32[32,128]{1,0:T(8,128)} %get-tuple-element.8) | data formatting | bytes 32768
  25.8 1.3 %copy.12 = f32[2048]{0:T(1024)} copy(f32[2048]{0:T(1024)} %bitcast.4) | data formatting | bytes 16384

commit v3 on v2

--- a/solution.py
+++ b/solution.py
@@ -24,7 +24,7 @@
     poles_hbm, parents_hbm, ops_hbm, l2l_hbm, target_hbm, leaf_hbm, basis_hbm,
     local_ref, pot_ref,
     ops_ref, l2l_ref, target_ref, leaf_ref, basis_ref,
-    gathered, elders, pieces, out_buf, in_buf, total, partials,
+    gathered, elders, window_ref, hot_ref, leaf_hot_ref, pieces, out_buf, in_buf, total, partials,
     load_sem, g_send, g_recv, e_send, e_recv, w_send, w_recv, p_send, p_recv,
 ):
     row = lax.axis_index("cells")
@@ -75,13 +75,6 @@
     for k in range(2):
         for d in range(1, n_coef):
             gather_copy(k, d, col).start()
-    loads[5].wait()
-    loads[0].wait()
-    for d in range(1, n_coef):
-        gather_copy(0, d, lax.rem(col + d, n_coef)).wait_recv()
-    loads[1].wait()
-
-    poles = jnp.concatenate([gathered[j] for j in range(n_coef)], axis=0)
     iota = lax.broadcasted_iota(jnp.int32, (cd, cd), 0).astype(jnp.float32).astype(jnp.bfloat16)
     one = jnp.ones((cd, cd), jnp.bfloat16)
     zero = jnp.zeros((cd, cd), jnp.bfloat16)
@@ -91,51 +84,77 @@
         tall = jnp.concatenate([wide] * (cd // 16), axis=0)
         return jnp.where(tall == iota, one, zero)
 
-    def lines(first, count):
-        result = []
-        for j in range(count):
-            line = target_ref[pl.ds(first + j, 1), :]
-            result.append(jnp.where(line >= 0, line - row * cd, -8 * REACH * cd))
-        return result
-
     def span(first, count):
         return pl.ds(pl.multiple_of(first * cd, cd), count * cd)
 
+    loads[0].wait()
+    targets = target_ref[...] - row * cd
+    window = targets // cd
+    window_ref[...] = jnp.where(target_ref[...] >= 0, window, 8 * REACH).astype(jnp.float32)
+    target_ref[...] = targets - window * cd
+
+    def fill(first, count):
+        hot_ref[:, span(first, count)] = jnp.concatenate(
+            [one_hot(target_ref[pl.ds(first + j, 1), :]) for j in range(count)], axis=1
+        )
+
+    full = noff // GROUP
+    lax.fori_loop(0, full, lambda i, _: fill(i * GROUP, GROUP), None)
+    if noff % GROUP:
+        fill(full * GROUP, noff % GROUP)
+
+    loads[3].wait()
+    leaf_hot_ref[...] = jnp.concatenate(
+        [one_hot(leaf_ref[t : t + 1, :] - row * cd) for t in range(tiles)], axis=1
+    )
+
+    loads[5].wait()
+    for d in range(1, n_coef):
+        gather_copy(0, d, lax.rem(col + d, n_coef)).wait_recv()
+    loads[1].wait()
+
+    poles = jnp.concatenate([gathered[j] for j in range(n_coef)], axis=0)
     def far(first, count):
         block = ops_ref[pl.ds(first, count)].reshape(count * share, width)
         terms = jnp.dot(block, poles, preferred_element_type=jnp.float32)
         high, low = halves(terms)
-        both = jnp.concatenate(
-            [
-                jnp.concatenate([part[j * share : (j + 1) * share] for j in range(count)], axis=1)
-                for part in (high, low)
-            ],
-            axis=0,
-        )
-        pieces[:, span(first, count)] = both
-        rows = lines(first, count)
-        hot = jnp.concatenate(
-            [
-                jnp.concatenate([one_hot(line - w * cd) for line in rows], axis=1)
-                for w in WINDOWS
-            ],
-            axis=0,
-        )
-        return lax.dot_general(both, hot, NT, preferred_element_type=jnp.float32)
+        both = [
+            jnp.concatenate([part[j * share : (j + 1) * share] for part in (high, low)], axis=0)
+            for j in range(count)
+        ]
+        pieces[:, span(first, count)] = jnp.concatenate(both, axis=1)
+        masked = [[] for _ in WINDOWS]
+        for j in range(count):
+            line = window_ref[pl.ds(first + j, 1), :]
+            wide = jnp.broadcast_to(line, (16, cd)).astype(jnp.bfloat16)
+            for i, w in enumerate(WINDOWS):
+                keep = jnp.where(wide == w, one[:16], zero[:16])
+                tall = jnp.concatenate([keep] * (2 * share // 16), axis=0)
+                masked[i].append(both[j] * tall)
+        stacked = jnp.concatenate([jnp.concatenate(m, axis=1) for m in masked], axis=0)
+        return lax.dot_general(
+            stacked, hot_ref[:, span(first, count)], NT, preferred_element_type=jnp.float32
+        )
 
     def near(first, count):
-        hot = jnp.concatenate([one_hot(line) for line in lines(first, count)], axis=1)
+        kept = []
+        for j in range(count):
+            line = window_ref[pl.ds(first + j, 1), :]
+            wide = jnp.broadcast_to(line, (16, cd)).astype(jnp.bfloat16)
+            keep = jnp.where(wide == 0, one[:16], zero[:16])
+            tall = jnp.concatenate([keep] * (2 * share // 16), axis=0)
+            kept.append(pieces[:, span(first + j, 1)] * tall)
         return lax.dot_general(
-            pieces[:, span(first, count)], hot, NT, preferred_element_type=jnp.float32
-        )
-
-    def over_offsets(step, columns):
-        full = noff // GROUP
-        acc = jnp.zeros((2 * share, columns), jnp.float32)
+            jnp.concatenate(kept, axis=1), hot_ref[:, span(first, count)], NT,
+            preferred_element_type=jnp.float32,
+        )
+
+    def over_offsets(step, rows):
+        acc = jnp.zeros((rows, cd), jnp.float32)
         acc = lax.fori_loop(0, full, lambda i, a: a + step(i * GROUP, GROUP), acc)
         if noff % GROUP:
             acc = acc + step(full * GROUP, noff % GROUP)
-        return acc[:share] + acc[share:]
+        return acc
 
     def window_copy(i, w):
         return pltpu.make_async_remote_copy(
@@ -144,15 +163,17 @@
             device_id=(row + w, col), device_id_type=pl.DeviceIdType.MESH,
         )
 
-    sums = over_offsets(far, len(WINDOWS) * cd)
+    sums = over_offsets(far, len(WINDOWS) * 2 * share)
     for i, w in enumerate(WINDOWS):
-        out_buf[i] = sums[:, i * cd : (i + 1) * cd]
+        base = 2 * share * i
+        out_buf[i] = sums[base : base + share] + sums[base + share : base + 2 * share]
     for i, w in enumerate(WINDOWS):
         @pl.when((row + w >= 0) & (row + w < n_cells))
         def _():
             window_copy(i, w).start()
 
-    total[...] = over_offsets(near, cd)
+    sums = over_offsets(near, 2 * share)
+    total[...] = sums[:share] + sums[share:]
 
     loads[2].wait()
     loads[6].wait()
@@ -178,10 +199,6 @@
     shifts = jnp.concatenate([l2l_ref[j] for j in range(8)], axis=1)
     total[...] += jnp.dot(shifts, spread, preferred_element_type=jnp.float32)
 
-    loads[3].wait()
-    leaf_hot = jnp.concatenate(
-        [one_hot(leaf_ref[t : t + 1, :] - row * cd) for t in range(tiles)], axis=1
-    )
     loads[4].wait()
 
     for i, w in enumerate(WINDOWS):
@@ -193,7 +210,7 @@
     local = total[...]
     local_ref[...] = local
     columns = jnp.dot(
-        jnp.concatenate(halves(local), axis=0), leaf_hot, preferred_element_type=jnp.float32
+        jnp.concatenate(halves(local), axis=0), leaf_hot_ref[...], preferred_element_type=jnp.float32
     )
     columns = columns[:share] + columns[share:]
     partial = jnp.sum(columns * basis_ref[...].astype(jnp.float32), axis=0, keepdims=True)
@@ -258,6 +275,9 @@
             pltpu.VMEM(particle_basis.shape, particle_basis.dtype),
             pltpu.VMEM((n_coef, share, cd), jnp.bfloat16),
             pltpu.VMEM((n_coef,) + parent_local.shape[::-1], jnp.bfloat16),
+            pltpu.VMEM(target_cell.shape, jnp.float32),
+            pltpu.VMEM((cd, noff * cd), jnp.bfloat16),
+            pltpu.VMEM((cd, particles), jnp.bfloat16),
             pltpu.VMEM((2 * share, noff * cd), jnp.bfloat16),
             pltpu.VMEM((nwin, share, cd), jnp.float32),
             pltpu.VMEM((nwin, share, cd), jnp.float32),

time: 27.4 us -> 24.2 us (0.88)
  Pallas kernels: 23.9 us -> 20.6 us
    pallas_call x1, Pallas kernels: 23.9 us -> 20.6 us  [on_device(): pl.pallas_call(functools.partial(kernel, n_cells, n_coef), out_shape=(jax...]
where the time goes in v3:
time: 24.2 us; the launch traced here: 23.8 us
  Pallas kernels  20.6 us (85%)
  local copies, waits for them, and re-layouts  2.62 us (11%)
  between operations  0.64 us (3%)
    pallas_call x1, Pallas kernels, on_device(): pl.pallas_call(functools.partial(kernel, n_cells, n_coef), out_shape=(jax...  20.6 us
    unnamed x2, local copies, waits for them, and re-layouts  2.62 us

profile of v3, /device:TPU:0, one launch (start us, length us, event | category | flops | bytes accessed | tf_op | source)
XLA Modules:
  0.0 23.8 jit_solution(12119011058331626364)
XLA Ops:
  0.6 20.6 %shard_map.86 = (f32[32,128]{1,0:T(8,128)}, f32[16,128]{1,0:T(8,128)}) custom-call(bf16[32,128]{1,0:T(8,128)(2,1)} %poles_hbm.1, bf16[16,32]{1,0:T(8,128)(2,1)} %bitcast.5, bf16[189,32,128]{2,1,0:T(8,128)(2,1)} %ops_hbm.1, bf16[8,32,128]{2,1,0:T(8,128)(2,1)} %l2l_hbm.1, s32[189,128]{1,0:T(8,128)} %target_hbm.1, s32[16,128]{1,0:T(8,128)} %bitcast.3, ...), custom_call_target="tpu_custom_call" | custom-call | tf_op jit(solution)/shard_map/pallas_call | solution.py:262
  21.2 1.3 %copy.11 = f32[32,128]{1,0:T(8,128)} copy(f32[32,128]{1,0:T(8,128)} %get-tuple-element.8) | data formatting | bytes 32768
  22.5 1.3 %copy.12 = f32[2048]{0:T(1024)} copy(f32[2048]{0:T(1024)} %bitcast.4) | data formatting | bytes 16384
